TPU v7x, 128 devices: a whole 4x4x4 slice. The times are simulated.
128 devices in a mesh: src: 8 (over x_lo, z), tgt: 16 (over y, x_hi, core).
Axes of the slice: x: 4 (x_hi: 2, x_lo: 2; x = x_hi * 2 + x_lo), y: 4, z: 4, core: 2. Of those that a mesh axis runs over, the one named last changes fastest.
Arguments:
- coeff: float32 [1024, 640, 256], P(('src', 'tgt')), may hold values from -6 to 6
- factors: float32 [3, 1024, 512, 256], P(None, ('src', 'tgt')), may hold values from -0.25 to 0.25
Outputs:
- result: float32 [1024, 640, 256], P('src', 'tgt')
All inputs are finite; a program needn't handle non-finite values.
Results may differ from a plain program's by a relative error of at most 0.0001.
Values sent between devices are 32-bit elements; how exact they have to be, the bound alone decides.
A program may use at most 128 MiB of HBM per device.

v0:
```python
import jax
import jax.numpy as jnp
from jax import lax
from jax.sharding import PartitionSpec as P


def partner_2(x, axis, bit):
    return lax.ppermute(x, axis, [(i, i ^ 1 << bit) for i in range(lax.axis_size(axis))])


def combine(coeff, partner, factor, upper):
    rank = coeff.shape[2]
    own_rows = lax.dynamic_slice_in_dim(factor, upper * rank, rank, 1)
    other_rows = lax.dynamic_slice_in_dim(factor, (1 - upper) * rank, rank, 1)
    first = jnp.einsum("nbr,nrk->nbk", coeff, own_rows, precision=lax.Precision.HIGHEST)
    second = jnp.einsum("nbr,nrk->nbk", partner, other_rows, precision=lax.Precision.HIGHEST)
    return first + second


def apply_level(coeff, factor, partner_of, upper):
    width = coeff.shape[1] // 2
    pieces = []
    for index in range(2):
        piece = coeff[:, index * width : (index + 1) * width]
        pieces.append(combine(piece, partner_of(piece), factor, upper))
    return jnp.concatenate(pieces, axis=1)


def local(coeff, factors):
    top_tgt = lax.axis_size("tgt").bit_length() - 2
    top_src = lax.axis_size("src").bit_length() - 2
    upper_first = lax.axis_index("tgt") >> top_tgt & 1
    upper_second = lax.axis_index("src") >> top_src & 1
    upper_third = lax.axis_index("tgt") & 1

    def partner_first(block):
        return partner_2(block, "tgt", top_tgt)

    def partner_second(block):
        return partner_2(block, "src", top_src)

    def partner_third(block):
        return partner_2(block, "tgt", 0)

    state = apply_level(coeff, factors[0], partner_first, upper_first)
    state = apply_level(state, factors[1], partner_second, upper_second)
    state = apply_level(state, factors[2], partner_third, upper_third)
    return lax.all_to_all(state, "tgt", split_axis=1, concat_axis=0, tiled=True)


def solution(mesh):
    placed = (P(("src", "tgt"), None, None), P(None, ("src", "tgt"), None, None))
    return jax.shard_map(
        local, mesh=mesh, in_specs=placed, out_specs=P("src", "tgt", None), check_vma=False
    )
```

profile of v0, /device:TPU:1, one launch (start us, length us, event | category | flops | bytes accessed | tf_op | source)
XLA Modules:
  0.0 296.3 jit_solution(18087775702369129488)
XLA Ops:
  0.0 5.3 %fusion.69 = (f32[8,320,256]{2,1,0:T(8,128)}, f32[8,320,256]{2,1,0:T(8,128)}) fusion(f32[8,640,256]{2,1,0:T(8,128)} %param.2), kind=kLoop, calls=%fused_computation.58 | loop fusion | bytes 10485760 | tf_op jit(solution)/shard_map/slice | solution.py:24
  5.3 3.7 %collective-permute-start = (f32[8,320,256]{2,1,0:T(8,128)}, f32[8,320,256]{2,1,0:T(8,128)}, u32[]{:S(2)}, u32[]{:S(2)}) collective-permute-start(f32[8,320,256]{2,1,0:T(8,128)} %get-tuple-element.8), channel_id=1, source_target_pairs={{0,8},{1,9},{2,10},{3,11},{4,12},{5,13},{6,14},{7,15},{8,0},{9,1},... | collective-permute-start | bytes 7864328 | tf_op jit(solution)/shard_map/ppermute | solution.py:8
  9.0 0.0 collective-permute-start.3
  9.1 9.3 %fusion.68 = (f32[1,8,512,256]{3,2,1,0:T(8,128)}, f32[1,8,512,256]{3,2,1,0:T(8,128)S(1)}, f32[1,8,512,256]{3,2,1,0:T(8,128)}) fusion(f32[3,8,512,256]{3,2,1,0:T(8,128)} %param.3), kind=kLoop, calls=%fused_computation.57 | loop fusion | bytes 25165824 | tf_op jit(solution)/shard_map/slice | solution.py:47
  18.4 0.0 copy-start.2
  18.4 4.7 %fusion.20 = f32[8,256,320]{1,2,0:T(8,128)S(1)} fusion(f32[1,8,512,256]{3,2,1,0:T(8,128)S(1)} %get-tuple-element.6, s32[]{:T(128)S(6)} %select_n.24, f32[8,640,256]{2,1,0:T(8,128)} %param.2), kind=kOutput, calls=%fused_computation.21 | convolution fusion | flops 2013265920 | bytes 7340036 | tf_op jit(solution)/shard_map/nbr,nrk->nbk/dot_general | solution.py:15
  23.1 0.0 copy-done.2
  23.1 3.0 fusion.22
  26.1 39.6 %collective-permute-done = f32[8,320,256]{2,1,0:T(8,128)} collective-permute-done((f32[8,320,256]{2,1,0:T(8,128)}, f32[8,320,256]{2,1,0:T(8,128)}, u32[]{:S(2)}, u32[]{:S(2)}) %collective-permute-start) | collective-permute-done | bytes 2621472 | tf_op jit(solution)/shard_map/ppermute | solution.py:8
  65.7 5.9 %fusion.36 = f32[8,256,320]{1,2,0:T(8,128)} fusion(f32[8,256,320]{1,2,0:T(8,128)S(1)} %fusion.22, f32[8,320,256]{2,1,0:T(8,128)} %collective-permute-done, f32[1,8,512,256]{3,2,1,0:T(8,128)S(1)} %get-tuple-element.6, s32[]{:T(128)S(6)} %select_n.25), kind=kOutput, calls=%fused_computation.37 | convolution fusion | flops 2013921280 | bytes 9961476 | tf_op jit(solution)/shard_map/nbr,nrk->nbk/dot_general | solution.py:16
  71.6 1.4 collective-permute-start.1
  73.1 48.8 %collective-permute-done.3 = f32[8,320,256]{2,1,0:T(8,128)} collective-permute-done((f32[8,320,256]{2,1,0:T(8,128)}, f32[8,320,256]{2,1,0:T(8,128)}, u32[]{:S(2)}, u32[]{:S(2)}) %collective-permute-start.3) | collective-permute-done | bytes 2621472 | tf_op jit(solution)/shard_map/ppermute | solution.py:8
  121.9 6.0 %fusion.39 = f32[8,256,320]{1,2,0:T(8,128)} fusion(f32[8,256,320]{1,2,0:T(8,128)S(1)} %fusion.20, f32[8,320,256]{2,1,0:T(8,128)} %collective-permute-done.3, f32[1,8,512,256]{3,2,1,0:T(8,128)S(1)} %get-tuple-element.6, s32[]{:T(128)S(6)} %select_n.25), kind=kOutput, calls=%fused_computation.38 | convolution fusion | flops 2013921280 | bytes 9961476 | tf_op jit(solution)/shard_map/nbr,nrk->nbk/dot_general | solution.py:16
  127.9 1.2 collective-permute-start.4
  129.1 0.0 copy-start.1
  129.1 5.1 %fusion.14 = f32[8,320,256]{2,1,0:T(8,128)S(1)} fusion(f32[8,256,320]{1,2,0:T(8,128)} %fusion.36, f32[1,8,512,256]{3,2,1,0:T(8,128)} %get-tuple-element.7, s32[]{:T(128)S(6)} %select_n.26), kind=kOutput, calls=%fused_computation.15 | convolution fusion | flops 2013265920 | bytes 7340036 | tf_op jit(solution)/shard_map/nbr,nrk->nbk/dot_general | solution.py:15
  134.2 0.0 copy-done.1
  134.2 4.3 %fusion.12 = f32[8,320,256]{2,1,0:T(8,128)S(1)} fusion(f32[8,256,320]{1,2,0:T(8,128)} %fusion.39, f32[1,8,512,256]{3,2,1,0:T(8,128)S(1)} %copy-done.1, s32[]{:T(128)S(6)} %select_n.26), kind=kOutput, calls=%fused_computation.13 | convolution fusion | flops 2013265920 | bytes 7340036 | tf_op jit(solution)/shard_map/nbr,nrk->nbk/dot_general | solution.py:15
  138.5 0.0 collective-permute-done.1
  138.6 4.4 %fusion.42 = f32[8,320,256]{2,1,0:T(8,128)S(1)} fusion(f32[8,320,256]{2,1,0:T(8,128)S(1)} %fusion.14, f32[8,320,256]{2,1,0:T(8,128)} %collective-permute-done.1, f32[1,8,512,256]{3,2,1,0:T(8,128)S(1)} %copy-done.1, s32[]{:T(128)S(6)} %select_n.27), kind=kOutput, calls=%fused_computation.39 | convolution fusion | flops 2013921280 | bytes 9961476 | tf_op jit(solution)/shard_map/nbr,nrk->nbk/dot_general | solution.py:16
  142.9 1.9 collective-permute-start.2
  144.8 40.6 %collective-permute-done.4 = f32[8,320,256]{2,1,0:T(8,128)} collective-permute-done((f32[8,320,256]{2,1,0:T(8,128)}, f32[8,320,256]{2,1,0:T(8,128)}, u32[]{:S(2)}, u32[]{:S(2)}) %collective-permute-start.4) | collective-permute-done | bytes 2621472 | tf_op jit(solution)/shard_map/ppermute | solution.py:8
  185.5 5.8 %fusion.45 = f32[8,320,256]{2,1,0:T(8,128)} fusion(f32[8,320,256]{2,1,0:T(8,128)S(1)} %fusion.12, f32[8,320,256]{2,1,0:T(8,128)} %collective-permute-done.4, f32[1,8,512,256]{3,2,1,0:T(8,128)S(1)} %copy-done.1, s32[]{:T(128)S(6)} %select_n.27), kind=kOutput, calls=%fused_computation.40 | convolution fusion | flops 2013921280 | bytes 9961476 | tf_op jit(solution)/shard_map/nbr,nrk->nbk/dot_general | solution.py:16
  191.3 10.7 %collective-permute-start.5 = (f32[8,320,256]{2,1,0:T(8,128)}, f32[8,320,256]{2,1,0:T(8,128)}, u32[]{:S(2)}, u32[]{:S(2)}) collective-permute-start(f32[8,320,256]{2,1,0:T(8,128)} %fusion.45), channel_id=1, source_target_pairs={{0,1},{1,0},{2,3},{3,2},{4,5},{5,4},{6,7},{7,6},{8,9},{9,8},{10,11... | collective-permute-start | bytes 7864328 | tf_op jit(solution)/shard_map/ppermute | solution.py:8
  201.9 0.0 copy-start
  201.9 4.4 %fusion.6 = f32[8,320,256]{2,1,0:T(8,128)S(1)} fusion(f32[8,320,256]{2,1,0:T(8,128)S(1)} %fusion.42, f32[1,8,512,256]{3,2,1,0:T(8,128)} %get-tuple-element.5, s32[]{:T(128)S(6)} %select_n.28), kind=kOutput, calls=%fused_computation.7 | convolution fusion | flops 2013265920 | bytes 7340036 | tf_op jit(solution)/shard_map/nbr,nrk->nbk/dot_general | solution.py:15
  206.3 0.0 copy-done
  206.3 4.3 %fusion.4 = f32[8,320,256]{2,1,0:T(8,128)S(1)} fusion(f32[8,320,256]{2,1,0:T(8,128)} %fusion.45, f32[1,8,512,256]{3,2,1,0:T(8,128)S(1)} %copy-done, s32[]{:T(128)S(6)} %select_n.28), kind=kOutput, calls=%fused_computation.5 | convolution fusion | flops 2013265920 | bytes 7340036 | tf_op jit(solution)/shard_map/nbr,nrk->nbk/dot_general | solution.py:15
  210.6 0.0 collective-permute-done.2
  210.7 4.6 %fusion.48 = f32[8,320,256]{2,1,0:T(8,128)S(1)} fusion(f32[8,320,256]{2,1,0:T(8,128)S(1)} %fusion.6, f32[8,320,256]{2,1,0:T(8,128)} %collective-permute-done.2, f32[1,8,512,256]{3,2,1,0:T(8,128)S(1)} %copy-done, s32[]{:T(128)S(6)} %select_n.29), kind=kOutput, calls=%fused_computation.41 | convolution fusion | flops 2013921280 | bytes 9961476 | tf_op jit(solution)/shard_map/nbr,nrk->nbk/dot_general | solution.py:16
  215.3 0.0 collective-permute-done.5
  215.3 4.6 %fusion.51 = f32[8,320,256]{2,1,0:T(8,128)S(1)} fusion(f32[8,320,256]{2,1,0:T(8,128)S(1)} %fusion.4, f32[8,320,256]{2,1,0:T(8,128)} %collective-permute-done.5, f32[1,8,512,256]{3,2,1,0:T(8,128)S(1)} %copy-done, s32[]{:T(128)S(6)} %select_n.29), kind=kOutput, calls=%fused_computation.42 | convolution fusion | flops 2013921280 | bytes 9961476 | tf_op jit(solution)/shard_map/nbr,nrk->nbk/dot_general | solution.py:16
  219.9 0.3 pad_maximum_fusion
  220.3 3.2 %copy.4 = f32[8,640,256]{2,0,1:T(8,128)S(1)} copy(f32[8,640,256]{2,1,0:T(8,128)S(1)} %pad_maximum_fusion) | data formatting | bytes 10485760 | tf_op jit(solution)/shard_map/concatenate | solution.py:26
  223.5 68.6 %all_to_all.18 = f32[8,640,256]{2,0,1:T(8,128)S(1)} all-to-all(f32[8,640,256]{2,0,1:T(8,128)S(1)} %copy.4), channel_id=1, replica_groups=mesh['src'=8,'tgt'=16] {'tgt'}, dimensions={1} | all-to-all | bytes 10485760 | tf_op jit(solution)/shard_map/all_to_all | solution.py:48
  292.1 4.0 %copy.5 = f32[16,8,40,256]{3,2,1,0:T(8,128)} copy(f32[16,8,40,256]{3,1,2,0:T(8,128)S(1)} %bitcast.58) | data formatting | bytes 10485760 | tf_op jit(solution)/shard_map/all_to_all | solution.py:48
Async XLA Ops:
  5.3 60.4 %collective-permute-start = (f32[8,320,256]{2,1,0:T(8,128)}, f32[8,320,256]{2,1,0:T(8,128)}, u32[]{:S(2)}, u32[]{:S(2)}) collective-permute-start(f32[8,320,256]{2,1,0:T(8,128)} %get-tuple-element.8), channel_id=1, source_target_pairs={{0,8},{1,9},{2,10},{3,11},{4,12},{5,13},{6,14},{7,15},{8,0},{9,1},... | collective-permute-start | bytes 7864328 | tf_op jit(solution)/shard_map/ppermute | solution.py:8
  9.0 112.8 %collective-permute-start.3 = (f32[8,320,256]{2,1,0:T(8,128)}, f32[8,320,256]{2,1,0:T(8,128)}, u32[]{:S(2)}, u32[]{:S(2)}) collective-permute-start(f32[8,320,256]{2,1,0:T(8,128)} %get-tuple-element.9), channel_id=1, source_target_pairs={{0,8},{1,9},{2,10},{3,11},{4,12},{5,13},{6,14},{7,15},{8,0},{9,1},... | collective-permute-start | bytes 7864328 | tf_op jit(solution)/shard_map/ppermute | solution.py:8
  18.4 4.7 %copy-start.2 = (f32[8,640,256]{2,1,0:T(8,128)S(1)}, f32[8,640,256]{2,1,0:T(8,128)}, u32[]{:S(2)}) copy-start(f32[8,640,256]{2,1,0:T(8,128)} %param.2) | copy-start | bytes 15728644
  71.6 66.9 %collective-permute-start.1 = (f32[8,320,256]{2,1,0:T(8,128)}, f32[8,320,256]{2,1,0:T(8,128)}, u32[]{:S(2)}, u32[]{:S(2)}) collective-permute-start(f32[8,320,256]{2,1,0:T(8,128)} %bitcast.3), channel_id=1, source_target_pairs={{0,64},{16,80},{32,96},{48,112},{64,0},{80,16},{96,32},{112,48},{1... | collective-permute-start | bytes 7864328 | tf_op jit(solution)/shard_map/ppermute | solution.py:8
  127.9 57.6 %collective-permute-start.4 = (f32[8,320,256]{2,1,0:T(8,128)}, f32[8,320,256]{2,1,0:T(8,128)}, u32[]{:S(2)}, u32[]{:S(2)}) collective-permute-start(f32[8,320,256]{2,1,0:T(8,128)} %bitcast.7), channel_id=1, source_target_pairs={{0,64},{16,80},{32,96},{48,112},{64,0},{80,16},{96,32},{112,48},{1... | collective-permute-start | bytes 7864328 | tf_op jit(solution)/shard_map/ppermute | solution.py:8
  129.1 5.1 %copy-start.1 = (f32[1,8,512,256]{3,2,1,0:T(8,128)S(1)}, f32[1,8,512,256]{3,2,1,0:T(8,128)}, u32[]{:S(2)}) copy-start(f32[1,8,512,256]{3,2,1,0:T(8,128)} %get-tuple-element.7) | copy-start | bytes 12582916
  142.9 67.7 %collective-permute-start.2 = (f32[8,320,256]{2,1,0:T(8,128)S(1)}, f32[8,320,256]{2,1,0:T(8,128)}, u32[]{:S(2)}, u32[]{:S(2)}) collective-permute-start(f32[8,320,256]{2,1,0:T(8,128)S(1)} %fusion.42), channel_id=1, source_target_pairs={{0,1},{1,0},{2,3},{3,2},{4,5},{5,4},{6,7},{7,6},{8,9},{9,8},{10,11... | collective-permute-start | bytes 7864328 | tf_op jit(solution)/shard_map/ppermute | solution.py:8
  191.3 24.0 %collective-permute-start.5 = (f32[8,320,256]{2,1,0:T(8,128)}, f32[8,320,256]{2,1,0:T(8,128)}, u32[]{:S(2)}, u32[]{:S(2)}) collective-permute-start(f32[8,320,256]{2,1,0:T(8,128)} %fusion.45), channel_id=1, source_target_pairs={{0,1},{1,0},{2,3},{3,2},{4,5},{5,4},{6,7},{7,6},{8,9},{9,8},{10,11... | collective-permute-start | bytes 7864328 | tf_op jit(solution)/shard_map/ppermute | solution.py:8
  201.9 4.4 %copy-start = (f32[1,8,512,256]{3,2,1,0:T(8,128)S(1)}, f32[1,8,512,256]{3,2,1,0:T(8,128)}, u32[]{:S(2)}) copy-start(f32[1,8,512,256]{3,2,1,0:T(8,128)} %get-tuple-element.5) | copy-start | bytes 12582916
where the time goes:
time: 300 us; the launch traced here: 296 us
  waiting for transfers between devices  129 us (43%)
  blocking collectives  68.6 us (23%)
  matrix products  57.1 us (19%)
  local copies, waits for them, and re-layouts  21.9 us (7%)
  starting transfers between devices  18.9 us (6%)
    ppermute x6, waiting for transfers between devices, partner_2(): lax.ppermute(x, axis, [(i, i ^ 1 << bit) for i in range(lax.axis_size(axi...  129 us
    all_to_all x1, blocking collectives, local(): return lax.all_to_all(state, 'tgt', split_axis=1, concat_axis=0, tiled=True)  68.6 us
    dot_general x6, matrix products, combine(): jnp.einsum('nbr,nrk->nbk', partner, other_rows, precision=lax.Precision.H...  31.3 us
    dot_general x6, matrix products, combine(): jnp.einsum('nbr,nrk->nbk', coeff, own_rows, precision=lax.Precision.HIGHEST)  25.8 us
    ppermute x6, starting transfers between devices, partner_2(): lax.ppermute(x, axis, [(i, i ^ 1 << bit) for i in range(lax.axis_size(axi...  18.9 us
    slice x1, local copies, waits for them, and re-layouts, local(): state = apply_level(state, factors[2], partner_third, upper_third)  9.3 us
  transfers between devices with their start and end apart: 6, of which 3 were waited for; matrix products, arithmetic and copies ran while one was open for 21% of the time, Pallas kernels for 0%

commit v1 on v0

v1 whole, which is shorter than its diff:
```python
import functools

import jax
import jax.numpy as jnp
from jax import lax
from jax.experimental import pallas as pl
from jax.experimental.pallas import tpu as pltpu
from jax.sharding import PartitionSpec as P

SPLIT = 4
AHEAD = 6
HOLD = 29
STEP = 0
MESH = pl.DeviceIdType.MESH


def split(x):
    high = x.astype(jnp.bfloat16)
    return high, (x - high.astype(jnp.float32)).astype(jnp.bfloat16)


def dot(x, w):
    x_high, x_low = split(x)
    w_high, w_low = split(w)
    mm = functools.partial(jnp.dot, preferred_element_type=jnp.float32)
    return mm(x_high, w_high) + (mm(x_high, w_low) + mm(x_low, w_high))


def kernel(
    n_src, n_tgt, coeff, factors, out,
    c_v, f_v, got0, got1, got2, new0, new1, new2,
    c_sem, f_sem, got0_sem, got1_sem, got2_sem, sent0, sent1, sent2, sent3, landed,
):
    blocks, rhs, rank = c_v.shape
    rows = rhs // SPLIT
    part = rhs // n_tgt
    count = blocks * SPLIT
    src = lax.axis_index("src")
    tgt = lax.axis_index("tgt")
    half_t, half_s = n_tgt // 2, n_src // 2
    upper = (tgt // half_t, src // half_s, lax.rem(tgt, 2))
    first = (src, lax.rem(tgt + half_t, n_tgt))
    second = (lax.rem(src + half_s, n_src), tgt)
    third = (src, tgt + 1 - 2 * lax.rem(tgt, 2))

    def load_c(block):
        return pltpu.make_async_copy(coeff.at[block], c_v.at[block], c_sem.at[block])

    def load_f(level, block):
        return pltpu.make_async_copy(
            factors.at[level, block], f_v.at[level, block], f_sem.at[level, block]
        )

    def place(chunk):
        block = chunk // SPLIT
        at = pl.multiple_of(lax.rem(chunk, SPLIT) * rows, rows)
        return block, pl.ds(at, rows)

    def exchange(source, target, sent, got, device, chunk):
        block, span = place(chunk)
        return pltpu.make_async_remote_copy(
            source.at[block, span, :], target.at[block, span, :], sent, got.at[chunk],
            device_id=device, device_id_type=MESH,
        )

    def exchange0(chunk):
        return exchange(coeff, got0, sent0, got0_sem, first, chunk)

    def exchange1(chunk):
        return exchange(new0, got1, sent1, got1_sem, second, chunk)

    def exchange2(chunk):
        return exchange(new1, got2, sent2, got2_sem, third, chunk)

    def combine(level, chunk, own, other, target):
        block, span = place(chunk)
        own_rows = pl.ds(pl.multiple_of(upper[level] * rank, rank), rank)
        other_rows = pl.ds(pl.multiple_of((1 - upper[level]) * rank, rank), rank)
        target[block, span, :] = dot(own[block, span, :], f_v[level, block, own_rows, :]) + dot(
            other[block, span, :], f_v[level, block, other_rows, :]
        )

    def scatter(block):
        out[tgt * blocks + block] = new2[block, pl.ds(pl.multiple_of(tgt * part, 8), part), :]

        @pl.loop(1, n_tgt)
        def _(k):
            to = lax.rem(tgt + k, n_tgt)
            pltpu.make_async_remote_copy(
                new2.at[block, pl.ds(pl.multiple_of(to * part, 8), part), :],
                out.at[tgt * blocks + block], sent3, landed,
                device_id=(src, to), device_id_type=MESH,
            ).start()

    @pl.loop(0, blocks)
    def _(block):
        load_c(block).start()
        load_f(0, block).start()

    barrier = pltpu.get_barrier_semaphore()

    @pl.loop(1, n_tgt)
    def _(k):
        pl.semaphore_signal(
            barrier, inc=1, device_id=(src, lax.rem(tgt + k, n_tgt)), device_id_type=MESH
        )

    pl.semaphore_signal(barrier, inc=1, device_id=second, device_id_type=MESH)
    pl.semaphore_wait(barrier, n_tgt)

    @pl.loop(0, AHEAD)
    def _(chunk):
        exchange0(chunk).start()

    @pl.loop(0, blocks)
    def _(block):
        load_f(1, block).start()
        load_f(2, block).start()

    @pl.loop(0, count + 2)
    def _(step):
        @pl.when(step + AHEAD < count)
        def _():
            exchange0(step + AHEAD).start()

        @pl.when(step < count)
        def _():
            block = step // SPLIT

            @pl.when(lax.rem(step, SPLIT) == 0)
            def _():
                load_c(block).wait()
                load_f(0, block).wait()

            exchange0(step).wait_recv()
            combine(0, step, c_v, got0, new0)
            exchange1(step).start()

        @pl.when((step >= 1) & (step < count + 1))
        def _():
            chunk = step - 1

            @pl.when(lax.rem(chunk, SPLIT) == 0)
            def _():
                load_f(1, chunk // SPLIT).wait()

            exchange1(chunk).wait_recv()
            combine(1, chunk, new0, got1, new1)
            exchange2(chunk).start()

        @pl.when(step >= 2)
        def _():
            chunk = step - 2

            @pl.when(lax.rem(chunk, SPLIT) == 0)
            def _():
                load_f(2, chunk // SPLIT).wait()

            exchange2(chunk).wait_recv()
            combine(2, chunk, new1, got2, new2)

        for block in range(blocks):
            ready = (block + 1) * SPLIT + 1

            @pl.when(step == max(ready, HOLD + STEP * block))
            def _(block=block):
                scatter(block)

    for copy in (
        pltpu.make_async_remote_copy(coeff, got0, sent0, landed, device_id=first, device_id_type=MESH),
        pltpu.make_async_remote_copy(new0, got1, sent1, landed, device_id=second, device_id_type=MESH),
        pltpu.make_async_remote_copy(new1, got2, sent2, landed, device_id=third, device_id_type=MESH),
    ):
        copy.wait_send()
    moved = out.at[pl.ds(0, (n_tgt - 1) * blocks)]
    last = pltpu.make_async_remote_copy(
        moved, moved, sent3, landed, device_id=third, device_id_type=MESH
    )
    last.wait_send()
    last.wait_recv()


def solution(mesh):
    n_src, n_tgt = mesh.shape["src"], mesh.shape["tgt"]

    def local(coeff, factors):
        blocks, rhs, rank = coeff.shape
        levels = factors.shape[0]
        count = blocks * SPLIT
        whole = pltpu.VMEM((blocks, rhs, rank), jnp.float32)
        dma = pltpu.SemaphoreType.DMA
        return pl.pallas_call(
            functools.partial(kernel, n_src, n_tgt),
            out_shape=jax.ShapeDtypeStruct((n_tgt * blocks, rhs // n_tgt, rank), jnp.float32),
            in_specs=[pl.BlockSpec(memory_space=pl.ANY)] * 2,
            out_specs=pl.BlockSpec(memory_space=pltpu.VMEM),
            scratch_shapes=[
                whole, pltpu.VMEM(factors.shape, jnp.float32), whole, whole, whole, whole, whole, whole,
                dma((blocks,)), dma((levels, blocks)), dma((count,)), dma((count,)), dma((count,)),
                dma, dma, dma, dma, dma,
            ],
            compiler_params=pltpu.CompilerParams(
                collective_id=0, has_side_effects=True, vmem_limit_bytes=60 * 1024 * 1024
            ),
        )(coeff, factors)

    placed = (P(("src", "tgt"), None, None), P(None, ("src", "tgt"), None, None))
    return jax.shard_map(
        local, mesh=mesh, in_specs=placed, out_specs=P("src", "tgt", None), check_vma=False
    )
```

time: 300 us -> 196 us (0.65); the launches traced: 296 us -> 196 us
  Pallas kernels: 0 us -> 191 us
  waiting for transfers between devices: 129 us -> 0 us
  blocking collectives: 68.6 us -> 0 us
  matrix products: 57.1 us -> 0 us
  starting transfers between devices: 18.9 us -> 0 us
  local copies, waits for them, and re-layouts: 21.9 us -> 5.18 us
    pallas_call x0 -> x1, Pallas kernels: none -> 191 us  [local(): pl.pallas_call(functools.partial(kernel, n_src, n_tgt), out_shape=jax.Sha...]
    ppermute x6 -> x0, waiting for transfers between devices: 129 us -> none  [partner_2(): lax.ppermute(x, axis, [(i, i ^ 1 << bit) for i in range(lax.axis_size(axi...]
    all_to_all x1 -> x0, blocking collectives: 68.6 us -> none  [local(): return lax.all_to_all(state, 'tgt', split_axis=1, concat_axis=0, tiled=True)]
    dot_general x12 -> x0, matrix products: 57.1 us -> none  [the longest x6 31.3 us: combine(): jnp.einsum('nbr,nrk->nbk', partner, other_rows, precision=lax.Precision.H...]
    ppermute x6 -> x0, starting transfers between devices: 18.9 us -> none  [partner_2(): lax.ppermute(x, axis, [(i, i ^ 1 << bit) for i in range(lax.axis_size(axi...]
    slice x2 -> x0, local copies, waits for them, and re-layouts: 14.6 us -> none  [the longest x1 9.3 us: local(): state = apply_level(state, factors[2], partner_third, upper_third)]
    unnamed x6 -> x1, local copies, waits for them, and re-layouts: 0.01 us -> 5.18 us
    all_to_all x1 -> x0, local copies, waits for them, and re-layouts: 3.99 us -> none  [local(): return lax.all_to_all(state, 'tgt', split_axis=1, concat_axis=0, tiled=True)]
  transfers between devices with their start and end apart: 6 -> 0, of which waited for: 3 -> 0; matrix products, arithmetic and copies ran while one was open for 21% -> 0% of each run, Pallas kernels for 0% -> 0%
where the time goes in v1:
time: 196 us
  Pallas kernels  191 us (97%)
  local copies, waits for them, and re-layouts  5.18 us (3%)
    pallas_call x1, Pallas kernels, local(): pl.pallas_call(functools.partial(kernel, n_src, n_tgt), out_shape=jax.Sha...  191 us
    unnamed x1, local copies, waits for them, and re-layouts  5.18 us

profile of v1, /device:TPU:1, one launch (start us, length us, event | category | flops | bytes accessed | tf_op | source)
XLA Modules:
  0.0 196.0 jit_solution(15258685801672381800)
XLA Ops:
  0.0 190.8 %shard_map.28 = f32[128,40,256]{2,1,0:T(8,128)} custom-call(f32[8,640,256]{2,1,0:T(8,128)} %coeff.1, f32[3,8,512,256]{3,2,1,0:T(8,128)} %factors.1), custom_call_target="tpu_custom_call" | custom-call | tf_op jit(solution)/shard_map/pallas_call | solution.py:192
  190.8 5.2 %copy.4 = f32[128,40,256]{2,1,0:T(8,128)} copy(f32[128,40,256]{2,1,0:T(8,128)} %shard_map.28) | data formatting | bytes 10485760

commit v2 on v1

--- a/solution.py
+++ b/solution.py
@@ -7,10 +7,12 @@
 from jax.experimental.pallas import tpu as pltpu
 from jax.sharding import PartitionSpec as P
 
-SPLIT = 4
-AHEAD = 6
-HOLD = 29
-STEP = 0
+SPLIT = 8
+AHEAD = 24
+LAG_B, LAG_C = 3, 5
+HOLD_Y, STEP_Y = 58, 1
+HOLD_XY, STEP_XY = 64, 0
+ORDER = (1, 3, 2)
 MESH = pl.DeviceIdType.MESH
 
 
@@ -64,13 +66,20 @@
         )
 
     def exchange0(chunk):
-        return exchange(coeff, got0, sent0, got0_sem, first, chunk)
+        return exchange(c_v, got0, sent0, got0_sem, first, chunk)
 
     def exchange1(chunk):
         return exchange(new0, got1, sent1, got1_sem, second, chunk)
 
     def exchange2(chunk):
         return exchange(new1, got2, sent2, got2_sem, third, chunk)
+
+    def send0(chunk):
+        @pl.when(lax.rem(chunk, SPLIT) == 0)
+        def _():
+            load_c(chunk // SPLIT).wait()
+
+        exchange0(chunk).start()
 
     def combine(level, chunk, own, other, target):
         block, span = place(chunk)
@@ -80,22 +89,33 @@
             other[block, span, :], f_v[level, block, other_rows, :]
         )
 
-    def scatter(block):
+    y, x, core = tgt // 4, lax.rem(tgt // 2, 2), lax.rem(tgt, 2)
+
+    def deliver(block, dy, other_x, other_core):
+        to_x = 1 - x if other_x else x
+        to_core = 1 - core if other_core else core
+        to = lax.rem(y + dy, n_tgt // 4) * 4 + to_x * 2 + to_core
+        pltpu.make_async_remote_copy(
+            new2.at[block, pl.ds(pl.multiple_of(to * part, 8), part), :],
+            out.at[tgt * blocks + block], sent3, landed,
+            device_id=(src, to), device_id_type=MESH,
+        ).start()
+
+    def scatter_x(block):
         out[tgt * blocks + block] = new2[block, pl.ds(pl.multiple_of(tgt * part, 8), part), :]
-
-        @pl.loop(1, n_tgt)
-        def _(k):
-            to = lax.rem(tgt + k, n_tgt)
-            pltpu.make_async_remote_copy(
-                new2.at[block, pl.ds(pl.multiple_of(to * part, 8), part), :],
-                out.at[tgt * blocks + block], sent3, landed,
-                device_id=(src, to), device_id_type=MESH,
-            ).start()
-
-    @pl.loop(0, blocks)
-    def _(block):
-        load_c(block).start()
-        load_f(0, block).start()
+        for other in (0, 1):
+            deliver(block, 0, 1, other)
+
+    def scatter_y(block):
+        for dy in ORDER:
+            for other in (0, 1):
+                deliver(block, dy, 0, other)
+        deliver(block, 0, 0, 1)
+
+    def scatter_xy(block):
+        for dy in ORDER:
+            for other in (0, 1):
+                deliver(block, dy, 1, other)
 
     barrier = pltpu.get_barrier_semaphore()
 
@@ -106,22 +126,30 @@
         )
 
     pl.semaphore_signal(barrier, inc=1, device_id=second, device_id_type=MESH)
+    load_c(0).start()
+    load_f(0, 0).start()
+
+    @pl.loop(1, blocks)
+    def _(block):
+        load_c(block).start()
+        load_f(0, block).start()
+
     pl.semaphore_wait(barrier, n_tgt)
 
     @pl.loop(0, AHEAD)
     def _(chunk):
-        exchange0(chunk).start()
+        send0(chunk)
 
     @pl.loop(0, blocks)
     def _(block):
         load_f(1, block).start()
         load_f(2, block).start()
 
-    @pl.loop(0, count + 2)
+    @pl.loop(0, count + LAG_C)
     def _(step):
         @pl.when(step + AHEAD < count)
         def _():
-            exchange0(step + AHEAD).start()
+            send0(step + AHEAD)
 
         @pl.when(step < count)
         def _():
@@ -129,16 +157,15 @@
 
             @pl.when(lax.rem(step, SPLIT) == 0)
             def _():
-                load_c(block).wait()
                 load_f(0, block).wait()
 
             exchange0(step).wait_recv()
             combine(0, step, c_v, got0, new0)
             exchange1(step).start()
 
-        @pl.when((step >= 1) & (step < count + 1))
-        def _():
-            chunk = step - 1
+        @pl.when((step >= LAG_B) & (step < count + LAG_B))
+        def _():
+            chunk = step - LAG_B
 
             @pl.when(lax.rem(chunk, SPLIT) == 0)
             def _():
@@ -148,9 +175,9 @@
             combine(1, chunk, new0, got1, new1)
             exchange2(chunk).start()
 
-        @pl.when(step >= 2)
-        def _():
-            chunk = step - 2
+        @pl.when(step >= LAG_C)
+        def _():
+            chunk = step - LAG_C
 
             @pl.when(lax.rem(chunk, SPLIT) == 0)
             def _():
@@ -160,14 +187,22 @@
             combine(2, chunk, new1, got2, new2)
 
         for block in range(blocks):
-            ready = (block + 1) * SPLIT + 1
-
-            @pl.when(step == max(ready, HOLD + STEP * block))
+            ready = (block + 1) * SPLIT - 1 + LAG_C
+
+            @pl.when(step == max(ready, HOLD_Y + STEP_Y * min(block, blocks - 2)))
             def _(block=block):
-                scatter(block)
+                scatter_y(block)
+
+            @pl.when(step == max(ready, HOLD_XY + STEP_XY * min(block, blocks - 2)))
+            def _(block=block):
+                scatter_xy(block)
+
+    @pl.loop(0, blocks)
+    def _(block):
+        scatter_x(block)
 
     for copy in (
-        pltpu.make_async_remote_copy(coeff, got0, sent0, landed, device_id=first, device_id_type=MESH),
+        pltpu.make_async_remote_copy(c_v, got0, sent0, landed, device_id=first, device_id_type=MESH),
         pltpu.make_async_remote_copy(new0, got1, sent1, landed, device_id=second, device_id_type=MESH),
         pltpu.make_async_remote_copy(new1, got2, sent2, landed, device_id=third, device_id_type=MESH),
     ):
@@ -180,6 +215,19 @@
     last.wait_recv()
 
 
+def store(source, out, sem):
+    pieces = 8
+    size = source.shape[0] // pieces
+    copies = [
+        pltpu.make_async_copy(source.at[pl.ds(i * size, size)], out.at[pl.ds(i * size, size)], sem.at[i])
+        for i in range(pieces)
+    ]
+    for copy in copies:
+        copy.start()
+    for copy in copies:
+        copy.wait()
+
+
 def solution(mesh):
     n_src, n_tgt = mesh.shape["src"], mesh.shape["tgt"]
 
@@ -189,9 +237,10 @@
         count = blocks * SPLIT
         whole = pltpu.VMEM((blocks, rhs, rank), jnp.float32)
         dma = pltpu.SemaphoreType.DMA
-        return pl.pallas_call(
+        shape = (n_tgt * blocks, rhs // n_tgt, rank)
+        landed = pl.pallas_call(
             functools.partial(kernel, n_src, n_tgt),
-            out_shape=jax.ShapeDtypeStruct((n_tgt * blocks, rhs // n_tgt, rank), jnp.float32),
+            out_shape=pltpu.VMEM(shape, jnp.float32),
             in_specs=[pl.BlockSpec(memory_space=pl.ANY)] * 2,
             out_specs=pl.BlockSpec(memory_space=pltpu.VMEM),
             scratch_shapes=[
@@ -200,9 +249,10 @@
                 dma, dma, dma, dma, dma,
             ],
             compiler_params=pltpu.CompilerParams(
-                collective_id=0, has_side_effects=True, vmem_limit_bytes=60 * 1024 * 1024
+                collective_id=0, has_side_effects=True, vmem_limit_bytes=54 * 1024 * 1024
             ),
         )(coeff, factors)
+        return landed
 
     placed = (P(("src", "tgt"), None, None), P(None, ("src", "tgt"), None, None))
     return jax.shard_map(

time: 196 us -> 186 us (0.949)
  Pallas kernels: 191 us -> 183 us
  local copies, waits for them, and re-layouts: 5.18 us -> 2.36 us
    pallas_call x1, Pallas kernels: 191 us -> 183 us  [local(): pl.pallas_call(functools.partial(kernel, n_src, n_tgt), out_shape=pltpu.V...]
    unnamed x1, local copies, waits for them, and re-layouts: 5.18 us -> 2.36 us
where the time goes in v2:
time: 186 us
  Pallas kernels  183 us (98%)
  local copies, waits for them, and re-layouts  2.36 us (1%)
    pallas_call x1, Pallas kernels, local(): pl.pallas_call(functools.partial(kernel, n_src, n_tgt), out_shape=pltpu.V...  183 us

profile of v2, /device:TPU:1, one launch (start us, length us, event | category | flops | bytes accessed | tf_op | source)
XLA Modules:
  0.0 185.6 jit_solution(2347399305229285553)
XLA Ops:
  0.0 183.2 %shard_map.28 = f32[128,40,256]{2,1,0:T(8,128)S(1)} custom-call(f32[8,640,256]{2,1,0:T(8,128)} %coeff.1, f32[3,8,512,256]{3,2,1,0:T(8,128)} %factors.1), custom_call_target="tpu_custom_call" | custom-call | tf_op jit(solution)/shard_map/pallas_call | solution.py:241
  183.2 2.4 %copy.4 = f32[128,40,256]{2,1,0:T(8,128)} copy(f32[128,40,256]{2,1,0:T(8,128)S(1)} %shard_map.28) | data formatting | bytes 10485760

commit v3 on v2

--- a/solution.py
+++ b/solution.py
@@ -31,7 +31,7 @@
 def kernel(
     n_src, n_tgt, coeff, factors, out,
     c_v, f_v, got0, got1, got2, new0, new1, new2,
-    c_sem, f_sem, got0_sem, got1_sem, got2_sem, sent0, sent1, sent2, sent3, landed,
+    c_sem, f_sem, got0_sem, got1_sem, got2_sem, sent0, sent1, sent2, sent3, landed, near, far,
 ):
     blocks, rhs, rank = c_v.shape
     rows = rhs // SPLIT
@@ -119,13 +119,14 @@
 
     barrier = pltpu.get_barrier_semaphore()
 
-    @pl.loop(1, n_tgt)
-    def _(k):
-        pl.semaphore_signal(
-            barrier, inc=1, device_id=(src, lax.rem(tgt + k, n_tgt)), device_id_type=MESH
-        )
-
-    pl.semaphore_signal(barrier, inc=1, device_id=second, device_id_type=MESH)
+    def greet(semaphore, device):
+        pl.semaphore_signal(semaphore, inc=1, device_id=device, device_id_type=MESH)
+
+    beside = (src, tgt + 2 - 4 * x)
+    for dy in (2, 1, 3):
+        greet(barrier, (src, lax.rem(tgt + 4 * dy, n_tgt)))
+    for device in (second, beside, third):
+        greet(barrier, device)
     load_c(0).start()
     load_f(0, 0).start()
 
@@ -134,7 +135,8 @@
         load_c(block).start()
         load_f(0, block).start()
 
-    pl.semaphore_wait(barrier, n_tgt)
+    pl.semaphore_wait(barrier, 6)
+    greet(near, third)
 
     @pl.loop(0, AHEAD)
     def _(chunk):
@@ -144,6 +146,10 @@
     def _(block):
         load_f(1, block).start()
         load_f(2, block).start()
+
+    pl.semaphore_wait(near, 1)
+    greet(far, beside)
+    pl.semaphore_wait(far, 1)
 
     @pl.loop(0, count + LAG_C)
     def _(step):
@@ -246,7 +252,7 @@
             scratch_shapes=[
                 whole, pltpu.VMEM(factors.shape, jnp.float32), whole, whole, whole, whole, whole, whole,
                 dma((blocks,)), dma((levels, blocks)), dma((count,)), dma((count,)), dma((count,)),
-                dma, dma, dma, dma, dma,
+                dma, dma, dma, dma, dma, pltpu.SemaphoreType.REGULAR, pltpu.SemaphoreType.REGULAR,
             ],
             compiler_params=pltpu.CompilerParams(
                 collective_id=0, has_side_effects=True, vmem_limit_bytes=54 * 1024 * 1024

time: 186 us -> 185 us (level)
  no operation moved by 1% of the time
where the time goes in v3:
time: 185 us
  Pallas kernels  183 us (99%)
  local copies, waits for them, and re-layouts  2.36 us (1%)
    pallas_call x1, Pallas kernels, local(): pl.pallas_call(functools.partial(kernel, n_src, n_tgt), out_shape=pltpu.V...  183 us

profile of v3, /device:TPU:1, one launch (start us, length us, event | category | flops | bytes accessed | tf_op | source)
XLA Modules:
  0.0 184.9 jit_solution(12495447837658628999)
XLA Ops:
  0.0 182.6 %shard_map.28 = f32[128,40,256]{2,1,0:T(8,128)S(1)} custom-call(f32[8,640,256]{2,1,0:T(8,128)} %coeff.1, f32[3,8,512,256]{3,2,1,0:T(8,128)} %factors.1), custom_call_target="tpu_custom_call" | custom-call | tf_op jit(solution)/shard_map/pallas_call | solution.py:247
  182.6 2.4 %copy.4 = f32[128,40,256]{2,1,0:T(8,128)} copy(f32[128,40,256]{2,1,0:T(8,128)S(1)} %shard_map.28) | data formatting | bytes 10485760

commit v4 on v3

--- a/solution.py
+++ b/solution.py
@@ -9,9 +9,10 @@
 
 SPLIT = 8
 AHEAD = 24
+FIRST = 3
 LAG_B, LAG_C = 3, 5
 HOLD_Y, STEP_Y = 58, 1
-HOLD_XY, STEP_XY = 64, 0
+HOLD_XY, STEP_XY = 54, 2
 ORDER = (1, 3, 2)
 MESH = pl.DeviceIdType.MESH
 
@@ -127,13 +128,9 @@
         greet(barrier, (src, lax.rem(tgt + 4 * dy, n_tgt)))
     for device in (second, beside, third):
         greet(barrier, device)
-    load_c(0).start()
+    for block in range(FIRST):
+        load_c(block).start()
     load_f(0, 0).start()
-
-    @pl.loop(1, blocks)
-    def _(block):
-        load_c(block).start()
-        load_f(0, block).start()
 
     pl.semaphore_wait(barrier, 6)
     greet(near, third)
@@ -141,6 +138,14 @@
     @pl.loop(0, AHEAD)
     def _(chunk):
         send0(chunk)
+
+    @pl.loop(1, blocks)
+    def _(block):
+        @pl.when(block >= FIRST)
+        def _():
+            load_c(block).start()
+
+        load_f(0, block).start()
 
     @pl.loop(0, blocks)
     def _(block):

time: 185 us -> 185 us (level)
  no operation moved by 1% of the time
where the time goes in v4:
time: 185 us
  Pallas kernels  182 us (98%)
  local copies, waits for them, and re-layouts  2.36 us (1%)
    pallas_call x1, Pallas kernels, local(): pl.pallas_call(functools.partial(kernel, n_src, n_tgt), out_shape=pltpu.V...  182 us

profile of v4, /device:TPU:1, one launch (start us, length us, event | category | flops | bytes accessed | tf_op | source)
XLA Modules:
  0.0 184.6 jit_solution(3052534481074232992)
XLA Ops:
  0.0 182.2 %shard_map.28 = f32[128,40,256]{2,1,0:T(8,128)S(1)} custom-call(f32[8,640,256]{2,1,0:T(8,128)} %coeff.1, f32[3,8,512,256]{3,2,1,0:T(8,128)} %factors.1), custom_call_target="tpu_custom_call" | custom-call | tf_op jit(solution)/shard_map/pallas_call | solution.py:252
  182.3 2.4 %copy.4 = f32[128,40,256]{2,1,0:T(8,128)} copy(f32[128,40,256]{2,1,0:T(8,128)S(1)} %shard_map.28) | data formatting | bytes 10485760

commit v5 on v4

--- a/solution.py
+++ b/solution.py
@@ -10,7 +10,7 @@
 SPLIT = 8
 AHEAD = 24
 FIRST = 3
-LAG_B, LAG_C = 3, 5
+LAG_B, LAG_C = 4, 6
 HOLD_Y, STEP_Y = 58, 1
 HOLD_XY, STEP_XY = 54, 2
 ORDER = (1, 3, 2)

time: 185 us -> 185 us (level)
  no operation moved by 1% of the time
where the time goes in v5:
time: 185 us
  Pallas kernels  182 us (98%)
  local copies, waits for them, and re-layouts  2.36 us (1%)
    pallas_call x1, Pallas kernels, local(): pl.pallas_call(functools.partial(kernel, n_src, n_tgt), out_shape=pltpu.V...  182 us

profile of v5, /device:TPU:1, one launch (start us, length us, event | category | flops | bytes accessed | tf_op | source)
XLA Modules:
  0.0 184.6 jit_solution(12647561938520524704)
XLA Ops:
  0.0 182.2 %shard_map.28 = f32[128,40,256]{2,1,0:T(8,128)S(1)} custom-call(f32[8,640,256]{2,1,0:T(8,128)} %coeff.1, f32[3,8,512,256]{3,2,1,0:T(8,128)} %factors.1), custom_call_target="tpu_custom_call" | custom-call | tf_op jit(solution)/shard_map/pallas_call | solution.py:252
  182.3 2.4 %copy.4 = f32[128,40,256]{2,1,0:T(8,128)} copy(f32[128,40,256]{2,1,0:T(8,128)S(1)} %shard_map.28) | data formatting | bytes 10485760
